TPU v7x, 32 devices: a whole 2x2x4 slice. The times are simulated.
32 devices in a mesh: outer: 4 (over z), inner: 8 (over y, x, core).
Axes of the slice: x: 2, y: 2, z: 4, core: 2. Of those that a mesh axis runs over, the one named last changes fastest.
Arguments:
- query_proj: bfloat16 [2048, 8192], P(('outer', 'inner')), may hold values from -8 to 8
- key_proj: bfloat16 [2048, 512], P(('outer', 'inner')), may hold values from -8 to 8
- value_proj: bfloat16 [2048, 512], P(('outer', 'inner')), may hold values from -6 to 6
- positions: int32 [2048], P(('outer', 'inner')), may hold values from 0 to 2047, each once
Outputs:
- attended: bfloat16 [2048, 8192], P(('outer', 'inner'))
Inputs may be any that keep to these rules, and one draw needn't show every extreme that they name: `positions`: each position from 0 to 2047 appears exactly once.
All inputs are finite; a program needn't handle non-finite values.
Results may differ from a plain program's by a relative error of at most 0.005.
Values may be sent and summed in bfloat16 or wider, within the bound.
A program may use at most 64 MiB of HBM per device.

v0:
```python
import functools
import math

import jax
import jax.numpy as jnp
from jax import lax
from jax.experimental import pallas as pl
from jax.experimental.pallas import tpu as pltpu
from jax.sharding import PartitionSpec as P

HEAD_WIDTH = 128
HIDDEN = -1e30


def kernel(sizes, q_ref, k_ref, v_ref, pos_ref, out_ref, buf, pbuf, mask, top, acc,
           q_buf, copy_sem, recv_sem, send_sem):
    nz, ny, nx, rows, heads_kv, group = sizes
    d = HEAD_WIDTH
    half_heads = heads_kv // 2
    wide = half_heads * d
    chips = ny * nx
    slots = 2 * chips
    keys = slots * rows
    z = lax.axis_index("outer")
    inner = lax.axis_index("inner")
    core = lax.rem(inner, 2)
    x = lax.rem(inner // 2, nx)
    y = inner // (2 * nx)

    def dev(dz=0, dy=0, dx=0, dc=0):
        zz = lax.rem(z + dz, nz)
        yy = lax.rem(y + dy, ny)
        xx = lax.rem(x + dx, nx)
        cc = lax.rem(core + dc, 2)
        return (zz, (yy * nx + xx) * 2 + cc)

    def slot(dx, dy, dc):
        return (dc * ny + dy) * nx + dx

    query_copy = pltpu.make_async_copy(q_ref, q_buf, copy_sem.at[5])
    local = []
    for half in range(2):
        cols = pl.ds(half * wide, wide)
        for part, ref in enumerate((k_ref, v_ref)):
            local.append(pltpu.make_async_copy(
                ref.at[:, cols], buf.at[0, half, 0, :, pl.ds(part * wide, wide)],
                copy_sem.at[2 * half + part]))
    local.append(pltpu.make_async_copy(pos_ref, pbuf.at[0, 0], copy_sem.at[4]))
    for c in local:
        c.start()

    query_copy.start()
    barrier = pltpu.get_barrier_semaphore()
    peers = [dict(dz=i) for i in sorted({1 % nz, nz - 1} - {0})] + [dict(dy=i) for i in range(1, ny)]
    peers += [dict(dx=i) for i in range(1, nx)] + [dict(dc=1)]
    for peer in peers:
        pl.semaphore_signal(barrier, inc=1, device_id=dev(**peer),
                            device_id_type=pl.DeviceIdType.MESH)
    pl.semaphore_wait(barrier, len(peers))
    for c in local:
        c.wait()

    sent = []

    def ref_of(s, kind, sl):
        return pbuf.at[s, sl] if kind == 2 else buf.at[s, kind, sl]

    def send(src, dst, to):
        n = len(sent)
        c = pltpu.make_async_remote_copy(
            src_ref=ref_of(*src), dst_ref=ref_of(*dst), send_sem=send_sem.at[n],
            recv_sem=recv_sem.at[dst[0], dst[1], dst[2]], device_id=dev(**to),
            device_id_type=pl.DeviceIdType.MESH)
        c.start()
        sent.append(c)

    def arrived(s, kind, sl):
        r = ref_of(s, kind, sl)
        pltpu.make_async_remote_copy(
            src_ref=r, dst_ref=r, send_sem=send_sem.at[0],
            recv_sem=recv_sem.at[s, kind, sl], device_id=dev(dc=1),
            device_id_type=pl.DeviceIdType.MESH).wait_recv()

    KINDS = (2, 0, 1)

    def forward(s, kind):
        return s < nz - s or (s == nz - s and kind != 1)

    def issue_column(s):
        for kind in KINDS:
            if s:
                arrived(s, kind, 0)
            src = (s, kind, 0)
            if s + 1 < nz and (s == 0 or forward(s, kind)) and forward(s + 1, kind):
                send(src, (s + 1, kind, 0), dict(dz=1))
            before = (s - 1) % nz
            if before and not (s and forward(s, kind)) and not forward(before, kind):
                send(src, (before, kind, 0), dict(dz=nz - 1))
            order = ("x", "y") if kind != 1 else ("y", "x")
            for axis in order:
                if axis == "x":
                    for dx in range(1, nx):
                        send(src, (s, kind, slot(dx, 0, 0)), dict(dx=dx))
                else:
                    for dy in range(1, ny):
                        send(src, (s, kind, slot(0, dy, 0)), dict(dy=dy))
            send(src, (s, kind, slot(0, 0, 1)), dict(dc=1))

    def to_sibling(s, kind, dx, dy):
        send((s, kind, slot(dx, dy, 0)), (s, kind, slot(dx, dy, 1)), dict(dc=1))

    def relay(s):
        for kind in (2, 0):
            for dx in range(1, nx):
                here = slot(dx, 0, 0)
                arrived(s, kind, here)
                for dy in range(1, ny):
                    send((s, kind, here), (s, kind, slot(dx, dy, 0)), dict(dy=dy))
                to_sibling(s, kind, dx, 0)
        for dy in range(1, ny):
            here = slot(0, dy, 0)
            arrived(s, 1, here)
            for dx in range(1, nx):
                send((s, 1, here), (s, 1, slot(dx, dy, 0)), dict(dx=dx))
            to_sibling(s, 1, 0, dy)
        for dx in range(1, nx):
            arrived(s, 1, slot(dx, 0, 0))
            to_sibling(s, 1, dx, 0)
        for kind in (2, 0):
            for dy in range(1, ny):
                arrived(s, kind, slot(0, dy, 0))
                to_sibling(s, kind, 0, dy)

    def gather_rest(s):
        for kind in KINDS:
            for dy in range(1, ny):
                for dx in range(1, nx):
                    arrived(s, kind, slot(dx, dy, 0))
                    to_sibling(s, kind, dx, dy)
        for kind in KINDS:
            for sl in range(chips, slots):
                arrived(s, kind, sl)

    def build_mask(s):
        mine = jnp.concatenate([pos_ref[...], pos_ref[...]], axis=1)
        mine = jnp.broadcast_to(mine.astype(jnp.float32), (rows, 2 * rows))
        for sl in range(slots):
            theirs = jnp.broadcast_to(pbuf[s, sl].astype(jnp.float32), (2 * rows, rows)).T
            mask[sl * rows:(sl + 1) * rows, :] = jnp.where(
                theirs > mine, HIDDEN, 0.0).astype(jnp.bfloat16)

    eye = (lax.broadcasted_iota(jnp.int32, (rows, 2 * rows), 0)
           == lax.broadcasted_iota(jnp.int32, (rows, 2 * rows), 1)).astype(jnp.bfloat16)
    scale = math.log2(math.e) / math.sqrt(d)
    per_tile = math.gcd(8, group)
    tile = per_tile * rows
    tiles = group // per_tile

    ones = jnp.ones((keys, d), jnp.bfloat16)

    def compute(n, s, half):
        @pl.loop(0, half_heads)
        def _(hh):
            head = half * half_heads + hh
            k_cols = pl.ds(pl.multiple_of(hh * d, d), d)
            v_cols = pl.ds(pl.multiple_of(wide + hh * d, d), d)
            k_wide = jnp.concatenate([buf[s, half, :, :, k_cols].reshape(keys, d), mask[...]],
                                     axis=1)
            v_wide = jnp.concatenate([buf[s, half, :, :, v_cols].reshape(keys, d), ones], axis=1)

            def columns(t, j):
                return pl.ds(pl.multiple_of((head * group + t * per_tile + j) * d, d), d)

            def score(t):
                query = jnp.concatenate(
                    [jnp.concatenate([q_buf[:, columns(t, j)], eye], axis=1)
                     for j in range(per_tile)], axis=0)
                return lax.dot_general(query, k_wide, (((1,), (1,)), ((), ())),
                                       preferred_element_type=jnp.float32)

            def fold(t, scores):
                window = slice(t * tile, (t + 1) * tile)
                new_top = jnp.broadcast_to(jnp.max(scores, axis=1, keepdims=True), (tile, d))
                if n:
                    old_top = top[head, window, :]
                    new_top = jnp.maximum(old_top, new_top)
                    rescale = jnp.exp2((old_top - new_top) * scale)
                weights = jnp.exp2((scores - jnp.concatenate([new_top] * (keys // d), axis=1)) * scale).astype(jnp.bfloat16)
                got = lax.dot_general(weights, v_wide, (((1,), (0,)), ((), ())),
                                      preferred_element_type=jnp.float32)
                if n:
                    got = acc[head, window, :] * jnp.concatenate([rescale, rescale], axis=1) + got
                if n < nz - 1:
                    acc[head, window, :] = got
                    top[head, window, :] = new_top
                else:
                    result = (got[:, :d] / got[:, d:]).astype(jnp.bfloat16)
                    for j in range(per_tile):
                        out_ref[:, columns(t, j)] = result[j * rows:(j + 1) * rows, :]

            held = score(0)
            for t in range(tiles):
                following = score(t + 1) if t + 1 < tiles else None
                fold(t, held)
                held = following

    plan = sorted(range(nz), key=lambda s: (min(s, nz - s), s))
    issue_column(0)
    relay(0)
    gather_rest(0)
    if nz > 1:
        issue_column(plan[1])
    query_copy.wait()
    for n, s in enumerate(plan):
        build_mask(s)
        if 0 < n < nz - 1:
            relay(plan[n + 1])
        compute(n, s, 0)
        if n == 0 and nz > 2:
            issue_column(plan[2])
        compute(n, s, 1)
        if n == 0 and nz > 1:
            relay(plan[1])
        if n + 3 < nz:
            issue_column(plan[n + 3])
        if n + 1 < nz:
            gather_rest(plan[n + 1])
    for c in sent:
        c.wait_send()


def body(query_proj, key_proj, value_proj, positions):
    rows, width = query_proj.shape
    d = HEAD_WIDTH
    heads_kv = key_proj.shape[1] // d
    group = width // d // heads_kv
    nz = lax.axis_size("outer")
    inner = lax.axis_size("inner")
    nx = 2
    ny = inner // 4
    slots = inner
    sizes = (nz, ny, nx, rows, heads_kv, group)
    wide = heads_kv // 2 * d
    copies = 3 * (nz - 1) + nz * (3 * (nx - 1 + ny - 1 + slots // 2) + 3 * (nx - 1) * (ny - 1))
    return pl.pallas_call(
        functools.partial(kernel, sizes),
        out_shape=jax.ShapeDtypeStruct((rows, width), jnp.bfloat16),
        in_specs=[pl.BlockSpec(memory_space=pl.ANY), pl.BlockSpec(memory_space=pl.ANY),
                  pl.BlockSpec(memory_space=pl.ANY), pl.BlockSpec(memory_space=pltpu.VMEM)],
        out_specs=pl.BlockSpec(memory_space=pltpu.VMEM),
        scratch_shapes=[
            pltpu.VMEM((nz, 2, slots, rows, 2 * wide), jnp.bfloat16),
            pltpu.VMEM((nz, slots, 1, rows), jnp.int32),
            pltpu.VMEM((slots * rows, d), jnp.bfloat16),
            pltpu.VMEM((heads_kv, group * rows, d), jnp.float32),
            pltpu.VMEM((heads_kv, group * rows, 2 * d), jnp.float32),
            pltpu.VMEM((rows, width), jnp.bfloat16),
            pltpu.SemaphoreType.DMA((6,)),
            pltpu.SemaphoreType.DMA((nz, 3, slots)),
            pltpu.SemaphoreType.DMA((copies,)),
        ],
        compiler_params=pltpu.CompilerParams(
            collective_id=0, has_side_effects=True, vmem_limit_bytes=44 * 1024 * 1024),
    )(query_proj, key_proj, value_proj, positions.reshape(1, rows))


def solution(mesh):
    return jax.shard_map(
        body,
        mesh=mesh,
        in_specs=(
            P(("outer", "inner"), None),
            P(("outer", "inner"), None),
            P(("outer", "inner"), None),
            P(("outer", "inner")),
        ),
        out_specs=P(("outer", "inner"), None),
        check_vma=False,
    )
```

profile of v0, /device:TPU:0, one launch (start us, length us, event | category | flops | bytes accessed | tf_op | source)
XLA Modules:
  0.0 45.6 jit_solution(4409344640633458891)
XLA Ops:
  0.0 0.0 copy-start.3
  0.0 0.7 %copy-done.3 = s32[64]{0:T(128)S(1)} copy-done((s32[64]{0:T(128)S(1)}, s32[64]{0:T(128)}, u32[]{:S(2)}) %copy-start.3) | copy-done | bytes 280
  0.7 0.0 copy-start
  0.7 1.2 %copy-done = bf16[64,8192]{1,0:T(8,128)(2,1)S(1)} copy-done((bf16[64,8192]{1,0:T(8,128)(2,1)S(1)}, bf16[64,8192]{1,0:T(8,128)(2,1)}, u32[]{:S(2)}) %copy-start) | copy-done | bytes 1048600
  1.9 0.0 copy-start.1
  1.9 0.8 %copy-done.1 = bf16[64,512]{1,0:T(8,128)(2,1)S(1)} copy-done((bf16[64,512]{1,0:T(8,128)(2,1)S(1)}, bf16[64,512]{1,0:T(8,128)(2,1)}, u32[]{:S(2)}) %copy-start.1) | copy-done | bytes 65560
  2.7 0.0 copy-start.2
  2.7 0.8 %copy-done.2 = bf16[64,512]{1,0:T(8,128)(2,1)S(1)} copy-done((bf16[64,512]{1,0:T(8,128)(2,1)S(1)}, bf16[64,512]{1,0:T(8,128)(2,1)}, u32[]{:S(2)}) %copy-start.2) | copy-done | bytes 65560
  3.6 41.1 %shard_map.46 = bf16[64,8192]{1,0:T(8,128)(2,1)S(1)} custom-call(bf16[64,8192]{1,0:T(8,128)(2,1)S(1)} %copy-done, bf16[64,512]{1,0:T(8,128)(2,1)S(1)} %copy-done.1, bf16[64,512]{1,0:T(8,128)(2,1)S(1)} %copy-done.2, s32[1,64]{1,0:T(1,128)S(1)} %bitcast.1), custom_call_target="tpu_custom_call" | custom-call | tf_op jit(solution)/shard_map/pallas_call | solution.py:245
  44.7 1.0 %copy.6 = bf16[64,8192]{1,0:T(8,128)(2,1)} copy(bf16[64,8192]{1,0:T(8,128)(2,1)S(1)} %shard_map.46) | data formatting | bytes 2097152
Async XLA Ops:
  0.0 0.7 %copy-start.3 = (s32[64]{0:T(128)S(1)}, s32[64]{0:T(128)}, u32[]{:S(2)}) copy-start(s32[64]{0:T(128)} %param.7) | copy-start | bytes 772
  0.7 1.2 %copy-start = (bf16[64,8192]{1,0:T(8,128)(2,1)S(1)}, bf16[64,8192]{1,0:T(8,128)(2,1)}, u32[]{:S(2)}) copy-start(bf16[64,8192]{1,0:T(8,128)(2,1)} %q_ref.1) | copy-start | bytes 3145732
  1.9 0.8 %copy-start.1 = (bf16[64,512]{1,0:T(8,128)(2,1)S(1)}, bf16[64,512]{1,0:T(8,128)(2,1)}, u32[]{:S(2)}) copy-start(bf16[64,512]{1,0:T(8,128)(2,1)} %k_ref.1) | copy-start | bytes 196612
  2.7 0.8 %copy-start.2 = (bf16[64,512]{1,0:T(8,128)(2,1)S(1)}, bf16[64,512]{1,0:T(8,128)(2,1)}, u32[]{:S(2)}) copy-start(bf16[64,512]{1,0:T(8,128)(2,1)} %v_ref.1) | copy-start | bytes 196612
where the time goes:
time: 45.9 us; the launch traced here: 45.6 us
  Pallas kernels  41.1 us (90%)
  local copies, waits for them, and re-layouts  4.53 us (10%)
    pallas_call x1, Pallas kernels, body(): pl.pallas_call(functools.partial(kernel, sizes), out_shape=jax.ShapeDtype...  41.1 us
    unnamed x9, local copies, waits for them, and re-layouts  4.53 us

commit v1 on v0

v1 whole, which is shorter than its diff:
```python
import functools
import math

import jax
import jax.numpy as jnp
from jax import lax
from jax.experimental import pallas as pl
from jax.experimental.pallas import tpu as pltpu
from jax.sharding import PartitionSpec as P

HEAD_WIDTH = 128
HIDDEN = -1e30
POS = 2
KINDS = (POS, 0, 1)
MESH = pl.DeviceIdType.MESH


def rank_of(p, s, nz):
    d = jnp.abs(s - p)
    m = jnp.minimum(p, nz - 1 - p)
    return jnp.where(d <= m, 2 * d - jnp.where(s < p, 1, 0), m + d)


def source_of(p, n, nz):
    m = jnp.minimum(p, nz - 1 - p)
    near = n <= 2 * m
    d = jnp.where(near, (n + 1) // 2, n - m)
    below = jnp.where(near, n % 2, jnp.where(p > nz - 1 - p, 1, 0))
    return p + d * (1 - 2 * below)


def kernel(sizes, q_ref, k_ref, v_ref, pos_ref, out_ref, buf, pbuf, other, mask, top, acc,
           q_buf, o_buf, copy_sem, recv_sem, q_sem, out_sem, send_sem):
    nz, ny, nx, rows, kinds, group = sizes
    d = HEAD_WIDTH
    chips = ny * nx
    both = 2 * rows
    keys = chips * both
    half = kinds * group * d
    z = lax.axis_index("outer")
    inner = lax.axis_index("inner")
    core = lax.rem(inner, 2)
    x = lax.rem(inner // 2, nx)
    y = inner // (2 * nx)

    def plane(dy=0, dx=0, dc=0, zz=None):
        yy = lax.rem(y + dy, ny)
        xx = lax.rem(x + dx, nx)
        cc = lax.rem(core + dc, 2)
        return (z if zz is None else zz, (yy * nx + xx) * 2 + cc)

    def slot(dx, dy):
        return dy * nx + dx

    local = []

    def fetch(src, dst):
        c = pltpu.make_async_copy(src, dst, copy_sem.at[len(local)])
        c.start()
        local.append(c)

    def head_cols(c, kind):
        return pl.ds(pl.multiple_of((c * kinds + kind) * d, d), d)

    for kind in range(kinds):
        for part, ref in enumerate((k_ref, v_ref)):
            cols = pl.ds(part * d, d)
            fetch(ref.at[:, head_cols(core, kind)], buf.at[0, kind, 0, pl.ds(0, rows), cols])
            fetch(ref.at[:, head_cols(1 - core, kind)], other.at[kind, :, cols])
    fetch(pos_ref, pbuf.at[0, 0, 0])
    early = len(local)
    my_cols = pl.ds(pl.multiple_of(core * half, half), half)
    their_cols = pl.ds(pl.multiple_of((1 - core) * half, half), half)
    fetch(q_ref.at[:, my_cols], q_buf.at[pl.ds(0, rows)])

    up, down = z + 1 < nz, z > 0
    barrier = pltpu.get_barrier_semaphore()

    def greet(where):
        pl.semaphore_signal(barrier, inc=1, device_id=where, device_id_type=MESH)

    fixed = 1
    greet(plane(dc=1))
    for dc in range(2):
        for dx in range(1, nx):
            greet(plane(dx=dx, dc=dc))
            fixed += 1
        for dy in range(1, ny):
            greet(plane(dy=dy, dc=dc))
            fixed += 1
        pl.when(up)(functools.partial(greet, plane(dc=dc, zz=z + 1)))
        pl.when(down)(functools.partial(greet, plane(dc=dc, zz=z - 1)))
    pl.semaphore_wait(barrier, fixed + 2 * (jnp.where(up, 1, 0) + jnp.where(down, 1, 0)))
    for c in local[:early]:
        c.wait()

    sent = []

    def ref_of(n, kind, sl, piece=None):
        if kind == POS:
            r = pbuf.at[n, sl]
            return r if piece is None else r.at[piece]
        r = buf.at[n, kind, sl]
        return r if piece is None else r.at[pl.ds(piece * rows, rows)]

    def send(src, dst, sem, to, when=None):
        c = pltpu.make_async_remote_copy(
            src_ref=src, dst_ref=dst, send_sem=send_sem.at[len(sent)], recv_sem=sem,
            device_id=to, device_id_type=MESH)
        sent.append((c, when))
        if when is None:
            c.start()
        else:
            pl.when(when)(c.start)

    def arrived(n, kind, sl):
        r = ref_of(n, kind, sl, None if n or sl else 1)
        pltpu.make_async_remote_copy(
            src_ref=r, dst_ref=r, send_sem=send_sem.at[0], recv_sem=recv_sem.at[n, kind, sl],
            device_id=plane(dc=1), device_id_type=MESH).wait_recv()

    def send_own(kind, n, sl, when=None, **to):
        send(ref_of(0, kind, 0, 0), ref_of(n, kind, sl, 0), recv_sem.at[n, kind, sl],
             plane(**to), when)
        mine = pbuf.at[0, 0, 0] if kind == POS else other.at[kind]
        send(mine, ref_of(n, kind, sl, 1), recv_sem.at[n, kind, sl], plane(dc=1, **to), when)

    def pass_on(kind, n, here, n_there, there, when=None, **to):
        send(ref_of(n, kind, here), ref_of(n_there, kind, there),
             recv_sem.at[n_there, kind, there], plane(**to), when)

    for kind in KINDS:
        mine = pbuf.at[0, 0, 0] if kind == POS else other.at[kind]
        send_own(kind, rank_of(z + 1, z, nz), 0, when=up, zz=z + 1)
        send_own(kind, rank_of(z - 1, z, nz), 0, when=down, zz=z - 1)
        for dx in range(1, nx):
            send_own(kind, 0, slot(dx, 0), dx=dx)
        for dy in range(1, ny):
            send_own(kind, 0, slot(0, dy), dy=dy)
        send(mine, ref_of(0, kind, 0, 1), recv_sem.at[0, kind, 0], plane(dc=1))
    send(q_ref.at[:, their_cols], q_buf.at[pl.ds(rows, rows)], q_sem, plane(dc=1))

    def along(n, kinds_now):
        source = source_of(z, n, nz)
        step = jnp.where(source < z, 1, -1)
        there = z + step
        more = jnp.logical_and(there >= 0, there < nz)
        for kind in kinds_now:
            pl.when(more)(functools.partial(arrived, n, kind, 0))
            pass_on(kind, n, 0, rank_of(there, source, nz), 0, when=more, zz=there)

    def across(n, kinds_now):
        source = source_of(z, n, nz)
        there = z + jnp.where(source < z, 1, -1)
        last = jnp.logical_or(there < 0, there >= nz)
        for kind in kinds_now:
            pl.when(last)(functools.partial(arrived, n, kind, 0))
            for dx in range(1, nx):
                pass_on(kind, n, 0, n, slot(dx, 0), dx=dx)
            for dy in range(1, ny):
                pass_on(kind, n, 0, n, slot(0, dy), dy=dy)

    def relay(n, kinds_now):
        for kind in kinds_now:
            if kind == 1:
                for dy in range(1, ny):
                    arrived(n, kind, slot(0, dy))
                    for dx in range(1, nx):
                        pass_on(kind, n, slot(0, dy), n, slot(dx, dy), dx=dx)
            else:
                for dx in range(1, nx):
                    arrived(n, kind, slot(dx, 0))
                    for dy in range(1, ny):
                        pass_on(kind, n, slot(dx, 0), n, slot(dx, dy), dy=dy)

    def gather(n, kinds_now):
        for kind in kinds_now:
            if n == 0:
                arrived(0, kind, 0)
            for dy in range(1, ny):
                if kind != 1:
                    arrived(n, kind, slot(0, dy))
            for dx in range(1, nx):
                if kind == 1:
                    arrived(n, kind, slot(dx, 0))
                for dy in range(1, ny):
                    arrived(n, kind, slot(dx, dy))

    def positions_of(n, sl):
        return jnp.concatenate([pbuf[n, sl, 0], pbuf[n, sl, 1]], axis=1).astype(jnp.float32)

    def build_mask(n):
        mine = jnp.broadcast_to(positions_of(0, 0), (both, both))
        for sl in range(chips):
            theirs = jnp.broadcast_to(positions_of(n, sl), (both, both)).T
            mask[n, sl * both:(sl + 1) * both, :] = jnp.where(
                theirs > mine, HIDDEN, 0.0).astype(jnp.bfloat16)

    eye = (lax.broadcasted_iota(jnp.int32, (both, both), 0)
           == lax.broadcasted_iota(jnp.int32, (both, both), 1)).astype(jnp.bfloat16)
    scale = math.log2(math.e) / math.sqrt(d)
    per_tile = math.gcd(max(1, 512 // both), group)
    tile = per_tile * both
    tiles = group // per_tile
    ones = jnp.ones((keys, d), jnp.bfloat16)

    def compute(n, kind):
        k_wide = jnp.concatenate([buf[n, kind, :, :, :d].reshape(keys, d), mask[n]], axis=1)
        v_wide = jnp.concatenate([buf[n, kind, :, :, d:].reshape(keys, d), ones], axis=1)

        def columns(t, j):
            at = (kind * group + t * per_tile + j) * d
            return slice(at, at + d)

        def score(t):
            query = jnp.concatenate(
                [jnp.concatenate([q_buf[:, columns(t, j)], eye], axis=1)
                 for j in range(per_tile)], axis=0)
            return lax.dot_general(query, k_wide, (((1,), (1,)), ((), ())),
                                   preferred_element_type=jnp.float32)

        def fold(t, scores):
            window = slice(t * tile, (t + 1) * tile)
            new_top = jnp.broadcast_to(jnp.max(scores, axis=1, keepdims=True), (tile, d))
            if n:
                old_top = top[kind, window, :]
                new_top = jnp.maximum(old_top, new_top)
                rescale = jnp.exp2((old_top - new_top) * scale)
            weights = jnp.exp2((scores - jnp.concatenate([new_top] * (keys // d), axis=1))
                               * scale).astype(jnp.bfloat16)
            got = lax.dot_general(weights, v_wide, (((1,), (0,)), ((), ())),
                                  preferred_element_type=jnp.float32)
            if n:
                got = acc[kind, window, :] * jnp.concatenate([rescale, rescale], axis=1) + got
            if n < nz - 1:
                acc[kind, window, :] = got
                top[kind, window, :] = new_top
                return
            result = (got[:, :d] / got[:, d:]).astype(jnp.bfloat16)
            for j in range(per_tile):
                o_buf[:, columns(t, j)] = result[j * both + rows:(j + 1) * both, :]
            for j in range(per_tile):
                at = columns(t, j).start
                out_ref[:, pl.ds(pl.multiple_of(core * half + at, d), d)] = (
                    result[j * both:j * both + rows, :])

        held = score(0)
        for t in range(tiles):
            following = score(t + 1) if t + 1 < tiles else None
            fold(t, held)
            held = following
        if n == nz - 1:
            wide = group * d
            send(o_buf.at[:, pl.ds(kind * wide, wide)],
                 out_ref.at[:, pl.ds(pl.multiple_of(core * half + kind * wide, wide), wide)],
                 out_sem.at[kind], plane(dc=1))

    first, second = (POS, 0), (1,)
    todo = [(n, ks) for n in range(nz) for ks in (first, second)]

    def ahead(i, what):
        if i < len(todo) and todo[i][0] > 0:
            what(*todo[i])

    def relay_at(i):
        if 0 <= i < len(todo):
            relay(*todo[i])

    ahead(2, along)
    ahead(4, along)
    ahead(2, across)
    relay_at(0)
    ahead(3, along)
    ahead(5, along)
    ahead(3, across)
    relay_at(1)
    ahead(6, along)
    ahead(4, across)
    relay_at(2)
    local[early].wait()
    pltpu.make_async_remote_copy(
        src_ref=q_buf.at[pl.ds(rows, rows)], dst_ref=q_buf.at[pl.ds(rows, rows)],
        send_sem=send_sem.at[0], recv_sem=q_sem, device_id=plane(dc=1),
        device_id_type=MESH).wait_recv()
    for i, (n, ks) in enumerate(todo):
        gather(n, ks)
        if POS in ks:
            build_mask(n)
        compute(n, ks[-1])
        ahead(i + 7, along)
        ahead(i + 5, across)
        relay_at(i + 3)
    wide = group * d
    for kind in range(kinds):
        r = out_ref.at[:, pl.ds(pl.multiple_of((1 - core) * half + kind * wide, wide), wide)]
        pltpu.make_async_remote_copy(
            src_ref=r, dst_ref=r, send_sem=send_sem.at[0], recv_sem=out_sem.at[kind],
            device_id=plane(dc=1), device_id_type=MESH).wait_recv()
    for c, when in sent:
        if when is None:
            c.wait_send()
        else:
            pl.when(when)(c.wait_send)


def body(query_proj, key_proj, value_proj, positions):
    rows, width = query_proj.shape
    d = HEAD_WIDTH
    heads_kv = key_proj.shape[1] // d
    group = width // d // heads_kv
    nz = lax.axis_size("outer")
    inner = lax.axis_size("inner")
    nx = 2
    ny = inner // (2 * nx)
    chips = ny * nx
    kinds = heads_kv // 2
    both = 2 * rows
    sizes = (nz, ny, nx, rows, kinds, group)
    near = nx - 1 + ny - 1
    copies = (6 * (near + 2) + 4 + 3 * (nz - 1) * (1 + near)
              + 3 * nz * (nx - 1) * (ny - 1) + kinds)
    hbm = pl.BlockSpec(memory_space=pltpu.HBM)
    operands = [pltpu.with_memory_space_constraint(a, pltpu.HBM) for a in (
        query_proj, key_proj, value_proj, positions.reshape(1, rows))]
    return pl.pallas_call(
        functools.partial(kernel, sizes),
        out_shape=pltpu.VMEM((rows, width), jnp.bfloat16),
        in_specs=[hbm, hbm, hbm, hbm],
        out_specs=pl.BlockSpec(memory_space=pltpu.VMEM),
        scratch_shapes=[
            pltpu.VMEM((nz, kinds, chips, both, 2 * d), jnp.bfloat16),
            pltpu.VMEM((nz, chips, 2, 1, rows), jnp.int32),
            pltpu.VMEM((kinds, rows, 2 * d), jnp.bfloat16),
            pltpu.VMEM((nz, chips * both, both), jnp.bfloat16),
            pltpu.VMEM((kinds, group * both, d), jnp.float32),
            pltpu.VMEM((kinds, group * both, 2 * d), jnp.float32),
            pltpu.VMEM((both, width // 2), jnp.bfloat16),
            pltpu.VMEM((rows, width // 2), jnp.bfloat16),
            pltpu.SemaphoreType.DMA((4 * kinds + 2,)),
            pltpu.SemaphoreType.DMA((nz, 3, chips)),
            pltpu.SemaphoreType.DMA,
            pltpu.SemaphoreType.DMA((kinds,)),
            pltpu.SemaphoreType.DMA((copies,)),
        ],
        compiler_params=pltpu.CompilerParams(
            collective_id=0, has_side_effects=True, vmem_limit_bytes=48 * 1024 * 1024),
    )(*operands)


def solution(mesh):
    return jax.shard_map(
        body,
        mesh=mesh,
        in_specs=(
            P(("outer", "inner"), None),
            P(("outer", "inner"), None),
            P(("outer", "inner"), None),
            P(("outer", "inner")),
        ),
        out_specs=P(("outer", "inner"), None),
        check_vma=False,
    )
```

time: 45.9 us -> 32.7 us (0.71)
  Pallas kernels: 41.1 us -> 31.5 us
  local copies, waits for them, and re-layouts: 4.53 us -> 0.97 us
    pallas_call x1, Pallas kernels: 41.1 us -> 31.5 us  [body(): pl.pallas_call(functools.partial(kernel, sizes), out_shape=pltpu.VMEM((ro...]
    unnamed x9 -> x1, local copies, waits for them, and re-layouts: 4.53 us -> 0.97 us
where the time goes in v1:
time: 32.7 us; the launch traced here: 32.5 us
  Pallas kernels  31.5 us (96%)
  local copies, waits for them, and re-layouts  0.97 us (3%)
    pallas_call x1, Pallas kernels, body(): pl.pallas_call(functools.partial(kernel, sizes), out_shape=pltpu.VMEM((ro...  31.5 us
    unnamed x1, local copies, waits for them, and re-layouts  0.97 us

profile of v1, /device:TPU:0, one launch (start us, length us, event | category | flops | bytes accessed | tf_op | source)
XLA Modules:
  0.0 32.5 jit_solution(1222122978381656895)
XLA Ops:
  0.0 31.5 %shard_map.46 = bf16[64,8192]{1,0:T(8,128)(2,1)S(1)} custom-call(bf16[64,8192]{1,0:T(8,128)(2,1)} %q_ref.1, bf16[64,512]{1,0:T(8,128)(2,1)} %k_ref.1, bf16[64,512]{1,0:T(8,128)(2,1)} %v_ref.1, s32[1,64]{1,0:T(1,128)} %bitcast.1), custom_call_target="tpu_custom_call" | custom-call | tf_op jit(solution)/shard_map/pallas_call | solution.py:325
  31.6 1.0 %copy.6 = bf16[64,8192]{1,0:T(8,128)(2,1)} copy(bf16[64,8192]{1,0:T(8,128)(2,1)S(1)} %shard_map.46) | data formatting | bytes 2097152

commit v2 on v1

v2 whole, which is shorter than its diff:
```python
import functools
import math

import jax
import jax.numpy as jnp
from jax import lax
from jax.experimental import pallas as pl
from jax.experimental.pallas import tpu as pltpu
from jax.sharding import PartitionSpec as P

HEAD_WIDTH = 128
HIDDEN = -1e30
PIECES = 4
POS = PIECES
MESH = pl.DeviceIdType.MESH


def rank_of(p, s, nz):
    d = jnp.abs(s - p)
    m = jnp.minimum(p, nz - 1 - p)
    return jnp.where(d <= m, 2 * d - jnp.where(s < p, 1, 0), m + d)


def source_of(p, n, nz):
    m = jnp.minimum(p, nz - 1 - p)
    near = n <= 2 * m
    d = jnp.where(near, (n + 1) // 2, n - m)
    below = jnp.where(near, n % 2, jnp.where(p > nz - 1 - p, 1, 0))
    return p + d * (1 - 2 * below)


def kernel(sizes, q_ref, k_ref, v_ref, pos_ref, out_ref, buf, pbuf, other, mask, top, acc,
           q_buf, o_buf, copy_sem, recv_sem, q_sem, out_sem, send_sem):
    nz, ny, nx, rows, kinds, group = sizes
    d = HEAD_WIDTH
    chips = ny * nx
    both = 2 * rows
    keys = chips * both
    half = kinds * group * d
    z = lax.axis_index("outer")
    inner = lax.axis_index("inner")
    core = lax.rem(inner, 2)
    x = lax.rem(inner // 2, nx)
    y = inner // (2 * nx)

    def plane(dy=0, dx=0, dc=0, zz=None):
        yy = lax.rem(y + dy, ny)
        xx = lax.rem(x + dx, nx)
        cc = lax.rem(core + dc, 2)
        return (z if zz is None else zz, (yy * nx + xx) * 2 + cc)

    def slot(dx, dy):
        return dy * nx + dx

    def fetch(src, dst, n):
        c = pltpu.make_async_copy(src, dst, copy_sem.at[n])
        c.start()
        return c

    def head_cols(c, kind):
        return pl.ds(pl.multiple_of((c * kinds + kind) * d, d), d)

    for piece in range(PIECES):
        ref = v_ref if piece % 2 else k_ref
        fetch(ref.at[:, head_cols(core, piece // 2)], buf.at[0, piece, 0, pl.ds(0, rows)], 0)
        fetch(ref.at[:, head_cols(1 - core, piece // 2)], other.at[piece], 0)
    pos_copy = fetch(pos_ref, pbuf.at[0, 0, 0], 1)
    my_cols = pl.ds(pl.multiple_of(core * half, half), half)
    their_cols = pl.ds(pl.multiple_of((1 - core) * half, half), half)
    q_copy = fetch(q_ref.at[:, my_cols], q_buf.at[pl.ds(0, rows)], 2)

    up, down = z + 1 < nz, z > 0
    barrier = pltpu.get_barrier_semaphore()

    def greet(where):
        pl.semaphore_signal(barrier, inc=1, device_id=where, device_id_type=MESH)

    fixed = 1
    greet(plane(dc=1))
    for dc in range(2):
        for dx in range(1, nx):
            greet(plane(dx=dx, dc=dc))
            fixed += 1
        for dy in range(1, ny):
            greet(plane(dy=dy, dc=dc))
            fixed += 1
        pl.when(up)(functools.partial(greet, plane(dc=dc, zz=z + 1)))
        pl.when(down)(functools.partial(greet, plane(dc=dc, zz=z - 1)))
    pl.semaphore_wait(barrier, fixed + 2 * (jnp.where(up, 1, 0) + jnp.where(down, 1, 0)))
    pos_copy.wait()
    pltpu.make_async_copy(buf.at[0, :, 0], buf.at[0, :, 0], copy_sem.at[0]).wait()

    groups = {}
    waited = set()
    half_way = min(2, nz - 1)

    def on_line(n, piece):
        return piece == PIECES - 1 and 0 < n <= half_way

    def x_first(n, piece):
        return (n + piece) % 2 == 0

    def ref_of(n, piece, sl, part=None):
        if piece == POS:
            r = pbuf.at[n, sl]
            return r if part is None else r.at[part]
        r = buf.at[n, piece, sl]
        return r if part is None else r.at[pl.ds(part * rows, rows)]

    def send(src, dst, sem, to, group, when=None):
        at, cond, copies = groups.setdefault(group, (len(groups), when, []))
        c = pltpu.make_async_remote_copy(
            src_ref=src, dst_ref=dst, send_sem=send_sem.at[at], recv_sem=sem,
            device_id=to, device_id_type=MESH)
        copies.append(math.prod(src.shape))
        if when is None:
            c.start()
        else:
            pl.when(when)(c.start)

    def all_sent():
        for (is_pos, *_), (at, cond, copies) in groups.items():
            lines = sum(copies) // (rows if is_pos else rows * d)
            if is_pos:
                r = pbuf.at[0, pl.ds(0, lines // 2)] if lines > 1 else pbuf.at[0, 0, 0]
            else:
                r = q_buf.at[pl.ds(0, rows), pl.ds(0, lines * d)]
            c = pltpu.make_async_remote_copy(
                src_ref=r, dst_ref=r, send_sem=send_sem.at[at], recv_sem=q_sem,
                device_id=plane(dc=1), device_id_type=MESH)
            if cond is None:
                c.wait_send()
            else:
                pl.when(cond)(c.wait_send)

    def landed(r, sem):
        pltpu.make_async_remote_copy(
            src_ref=r, dst_ref=r, send_sem=send_sem.at[0], recv_sem=sem,
            device_id=plane(dc=1), device_id_type=MESH).wait_recv()

    def arrived(n, piece, sl):
        if (n, piece, sl) not in waited:
            waited.add((n, piece, sl))
            landed(ref_of(n, piece, sl, 1 if n == sl == 0 else None), recv_sem.at[n, piece, sl])

    def arrived_if(when, n, piece, sl):
        pl.when(when)(lambda: landed(ref_of(n, piece, sl), recv_sem.at[n, piece, sl]))

    def pass_on(name, n, piece, here, there, n_there=None, when=None, **to):
        n_there = n if n_there is None else n_there
        send(ref_of(n, piece, here), ref_of(n_there, piece, there),
             recv_sem.at[n_there, piece, there], plane(**to), (piece == POS, name, n), when)

    def send_own(name, piece, n, sl, when=None, **to):
        group = (piece == POS, name)
        send(ref_of(0, piece, 0, 0), ref_of(n, piece, sl, 0), recv_sem.at[n, piece, sl],
             plane(**to), group, when)
        mine = pbuf.at[0, 0, 0] if piece == POS else other.at[piece]
        send(mine, ref_of(n, piece, sl, 1), recv_sem.at[n, piece, sl], plane(dc=1, **to), group,
             when)

    for piece in (POS, *range(PIECES)):
        send_own("up", piece, rank_of(z + 1, z, nz), 0, when=up, zz=z + 1)
        send_own("down", piece, rank_of(z - 1, z, nz), 0, when=down, zz=z - 1)
        for dx in range(1, nx):
            send_own("plane", piece, 0, slot(dx, 0), dx=dx)
        for dy in range(1, ny):
            send_own("plane", piece, 0, slot(0, dy), dy=dy)
        mine = pbuf.at[0, 0, 0] if piece == POS else other.at[piece]
        send(mine, ref_of(0, piece, 0, 1), recv_sem.at[0, piece, 0], plane(dc=1),
             (piece == POS, "chip"))
        if piece == 1:
            send(q_ref.at[:, their_cols], q_buf.at[pl.ds(rows, rows)], q_sem, plane(dc=1),
                 (False, "queries"))

    def onward(n):
        source = source_of(z, n, nz)
        there = z + jnp.where(source < z, 1, -1)
        more = jnp.logical_and(there >= 0, there < nz)
        return there, rank_of(there, source, nz), more

    def along(n, piece):
        there, n_there, more = onward(n)
        arrived_if(more, n, piece, 0)
        pass_on("along", n, piece, 0, 0, n_there, more, zz=there)

    def across(n, piece):
        _, _, more = onward(n)
        arrived_if(jnp.logical_not(more), n, piece, 0)
        if not on_line(n, piece):
            for dx in range(1, nx):
                pass_on("across", n, piece, 0, slot(dx, 0), dx=dx)
            for dy in range(1, ny):
                pass_on("across", n, piece, 0, slot(0, dy), dy=dy)

    def relay(n, piece):
        if on_line(n, piece):
            return
        for dx in range(1, nx):
            for dy in range(1, ny):
                if x_first(n, piece):
                    arrived(n, piece, slot(dx, 0))
                    pass_on("relay", n, piece, slot(dx, 0), slot(dx, dy), dy=dy)
                else:
                    arrived(n, piece, slot(0, dy))
                    pass_on("relay", n, piece, slot(0, dy), slot(dx, dy), dx=dx)

    along_x = [slot(dx, 0) for dx in range(1, nx)]
    along_y = [slot(0, dy) for dy in range(1, ny)]
    corner = [slot(dx, dy) for dx in range(1, nx) for dy in range(1, ny)]

    def farther(n):
        there, n_there, more = onward(n)
        return there, n_there, jnp.logical_and(more, n_there <= half_way)

    def values(n, slots):
        last = PIECES - 1
        for sl in slots:
            if n == 0:
                arrived(0, last, sl)
                for name, there, when in (("values up", z + 1, up), ("values down", z - 1, down)):
                    pass_on(name, 0, last, sl, sl, rank_of(there, z, nz), when, zz=there)
            elif n <= half_way:
                there, n_there, more = farther(n)
                arrived_if(more, n, last, sl)
                pass_on("values", n, last, sl, sl, n_there, more, zz=there)

    def gather(n, piece):
        for sl in ([0] if n == 0 else []) + along_x + along_y + corner:
            if on_line(n, piece):
                arrived_if(jnp.logical_not(farther(n)[2]), n, piece, sl)
            else:
                arrived(n, piece, sl)

    def positions_of(n, sl):
        return jnp.concatenate([pbuf[n, sl, 0], pbuf[n, sl, 1]], axis=1).astype(jnp.float32)

    def build_mask(n):
        mine = jnp.broadcast_to(positions_of(0, 0), (both, both))
        for sl in range(chips):
            theirs = jnp.broadcast_to(positions_of(n, sl), (both, both)).T
            mask[n, sl * both:(sl + 1) * both, :] = jnp.where(
                theirs > mine, HIDDEN, 0.0).astype(jnp.bfloat16)

    def pick(owner):
        at = lax.broadcasted_iota(jnp.int32, (rows, both), 0) + owner * rows
        return (at == lax.broadcasted_iota(jnp.int32, (rows, both), 1)).astype(jnp.bfloat16)

    picks = [pick(0), pick(1)]
    scale = math.log2(math.e) / math.sqrt(d)
    per_tile = math.gcd(max(1, 512 // rows), group)
    tile = per_tile * rows
    tiles = [(owner, t) for owner in (1, 0) for t in range(group // per_tile)]
    ones = jnp.ones((keys, d), jnp.bfloat16)

    def column(kind, t, j):
        return (kind * group + t * per_tile + j) * d

    def score(n, kind, i):
        owner, t = tiles[i]
        k_wide = jnp.concatenate([buf[n, 2 * kind].reshape(keys, d), mask[n]], axis=1)
        query = jnp.concatenate(
            [jnp.concatenate([q_buf[owner * rows:(owner + 1) * rows,
                                    column(kind, t, j):column(kind, t, j) + d], picks[owner]],
                             axis=1)
             for j in range(per_tile)], axis=0)
        return lax.dot_general(query, k_wide, (((1,), (1,)), ((), ())),
                               preferred_element_type=jnp.float32)

    def fold(n, kind, i, scores):
        owner, t = tiles[i]
        v_wide = jnp.concatenate([buf[n, 2 * kind + 1].reshape(keys, d), ones], axis=1)
        window = slice(i * tile, (i + 1) * tile)
        new_top = jnp.broadcast_to(jnp.max(scores, axis=1, keepdims=True), (tile, d))
        if n:
            old_top = top[kind, window, :]
            new_top = jnp.maximum(old_top, new_top)
            rescale = jnp.exp2((old_top - new_top) * scale)
        weights = jnp.exp2((scores - jnp.concatenate([new_top] * (keys // d), axis=1))
                           * scale).astype(jnp.bfloat16)
        got = lax.dot_general(weights, v_wide, (((1,), (0,)), ((), ())),
                              preferred_element_type=jnp.float32)
        if n:
            got = acc[kind, window, :] * jnp.concatenate([rescale, rescale], axis=1) + got
        if n < nz - 1:
            acc[kind, window, :] = got
            top[kind, window, :] = new_top
            return
        result = (got[:, :d] / got[:, d:]).astype(jnp.bfloat16)
        for j in range(per_tile):
            at = column(kind, t, j)
            if owner:
                o_buf[:, at:at + d] = result[j * rows:(j + 1) * rows, :]
            else:
                out_ref[:, pl.ds(pl.multiple_of(core * half + at, d), d)] = (
                    result[j * rows:(j + 1) * rows, :])

    wide = group * d

    def swap(kind):
        send(o_buf.at[:, pl.ds(kind * wide, wide)],
             out_ref.at[:, pl.ds(pl.multiple_of(core * half + kind * wide, wide), wide)],
             out_sem.at[kind], plane(dc=1), (False, "out", kind))

    def at(what, n, pieces):
        if n < nz and (n or what is relay):
            for piece in pieces:
                if piece == 0:
                    what(n, POS)
                what(n, piece)

    def ready(i):
        n, kind = divmod(i, 2)
        for piece in ((POS, 0, 1), (2, 3))[kind]:
            gather(n, piece)
        if kind == 0:
            build_mask(n)

    def line_values(n, slots):
        if n <= half_way:
            values(n, slots)

    def between(i):
        if i == 0:
            at(along, 3, (3,))
            at(relay, 1, (3,))
            values(0, corner)
            at(across, 3, (0, 1))
            at(relay, 2, (0, 1))
            line_values(1, along_x + along_y)
        if i == 1:
            at(across, 3, (2, 3))
            at(relay, 2, (2, 3))
            line_values(2, along_x + along_y)
            line_values(1, corner)
        if i == 2:
            at(relay, 3, (0, 1))
            line_values(2, corner)
        if i == 3:
            at(relay, 3, (2, 3))
        if i % 2:
            for what in (along, across, relay):
                at(what, i // 2 + 4, range(PIECES))

    for piece in range(PIECES):
        at(along, 1, (piece,))
        at(across, 1, (piece,))
        at(along, 2, (piece,))
        at(relay, 0, (piece,))
    for piece in range(PIECES - 1):
        at(across, 2, (piece,))
        at(along, 3, (piece,))
        at(relay, 1, (piece,))
        if piece:
            values(0, along_y if piece == 1 else along_x)
    at(across, 2, (PIECES - 1,))
    q_copy.wait()
    landed(q_buf.at[pl.ds(rows, rows)], q_sem)

    ours = len(tiles) // 2
    work = [(n, kind, i) for n in range(nz - 1) for kind in range(2) for i in range(len(tiles))]
    last = [(kind, i) for kind in range(2) for i in range(len(tiles))]
    late = [(0, len(tiles) - 1)] + [(1, i) for i in range(ours, len(tiles))]
    work += [(nz - 1,) + w for w in last if w not in late] + [(nz - 1,) + w for w in late]
    begun = 0
    ready(0)
    held = score(*work[0])
    for w, task in enumerate(work):
        following = None
        if w + 1 < len(work):
            step = 2 * work[w + 1][0] + work[w + 1][1]
            if step > begun:
                between(begun)
                begun = step
                ready(step)
                if step == 2 * nz - 1:
                    swap(0)
            if work[w + 1] == (nz - 1,) + late[1]:
                swap(1)
            following = score(*work[w + 1])
        fold(*task, held)
        held = following
    for kind in range(kinds):
        start = pl.multiple_of((1 - core) * half + kind * wide, wide)
        landed(out_ref.at[:, pl.ds(start, wide)], out_sem.at[kind])
    all_sent()


def body(query_proj, key_proj, value_proj, positions):
    rows, width = query_proj.shape
    d = HEAD_WIDTH
    heads_kv = key_proj.shape[1] // d
    group = width // d // heads_kv
    nz = lax.axis_size("outer")
    inner = lax.axis_size("inner")
    nx = 2
    ny = inner // (2 * nx)
    chips = ny * nx
    kinds = heads_kv // 2
    both = 2 * rows
    sizes = (nz, ny, nx, rows, kinds, group)
    groups = 11 + 4 * (nz - 1) + 2 * nz + min(2, nz - 1) + kinds
    hbm = pl.BlockSpec(memory_space=pltpu.HBM)
    operands = [pltpu.with_memory_space_constraint(a, pltpu.HBM) for a in (
        query_proj, key_proj, value_proj, positions.reshape(1, rows))]
    return pl.pallas_call(
        functools.partial(kernel, sizes),
        out_shape=pltpu.VMEM((rows, width), jnp.bfloat16),
        in_specs=[hbm, hbm, hbm, hbm],
        out_specs=pl.BlockSpec(memory_space=pltpu.VMEM),
        scratch_shapes=[
            pltpu.VMEM((nz, PIECES, chips, both, d), jnp.bfloat16),
            pltpu.VMEM((nz, chips, 2, 1, rows), jnp.int32),
            pltpu.VMEM((PIECES, rows, d), jnp.bfloat16),
            pltpu.VMEM((nz, chips * both, both), jnp.bfloat16),
            pltpu.VMEM((kinds, group * both, d), jnp.float32),
            pltpu.VMEM((kinds, group * both, 2 * d), jnp.float32),
            pltpu.VMEM((both, width // 2), jnp.bfloat16),
            pltpu.VMEM((rows, width // 2), jnp.bfloat16),
            pltpu.SemaphoreType.DMA((3,)),
            pltpu.SemaphoreType.DMA((nz, PIECES + 1, chips)),
            pltpu.SemaphoreType.DMA,
            pltpu.SemaphoreType.DMA((kinds,)),
            pltpu.SemaphoreType.DMA((groups,)),
        ],
        compiler_params=pltpu.CompilerParams(
            collective_id=0, has_side_effects=True, vmem_limit_bytes=48 * 1024 * 1024),
    )(*operands)


def solution(mesh):
    return jax.shard_map(
        body,
        mesh=mesh,
        in_specs=(
            P(("outer", "inner"), None),
            P(("outer", "inner"), None),
            P(("outer", "inner"), None),
            P(("outer", "inner")),
        ),
        out_specs=P(("outer", "inner"), None),
        check_vma=False,
    )
```

time: 32.7 us -> 30.2 us (0.924)
  Pallas kernels: 31.5 us -> 29.1 us
    pallas_call x1, Pallas kernels: 31.5 us -> 29.1 us  [body(): pl.pallas_call(functools.partial(kernel, sizes), out_shape=pltpu.VMEM((ro...]
where the time goes in v2:
time: 30.2 us; the launch traced here: 30.1 us
  Pallas kernels  29.1 us (96%)
  local copies, waits for them, and re-layouts  0.97 us (3%)
    pallas_call x1, Pallas kernels, body(): pl.pallas_call(functools.partial(kernel, sizes), out_shape=pltpu.VMEM((ro...  29.1 us
    unnamed x1, local copies, waits for them, and re-layouts  0.97 us

profile of v2, /device:TPU:0, one launch (start us, length us, event | category | flops | bytes accessed | tf_op | source)
XLA Modules:
  0.0 30.1 jit_solution(5648855608000400027)
XLA Ops:
  0.0 29.1 %shard_map.46 = bf16[64,8192]{1,0:T(8,128)(2,1)S(1)} custom-call(bf16[64,8192]{1,0:T(8,128)(2,1)} %q_ref.1, bf16[64,512]{1,0:T(8,128)(2,1)} %k_ref.1, bf16[64,512]{1,0:T(8,128)(2,1)} %v_ref.1, s32[1,64]{1,0:T(1,128)} %bitcast.1), custom_call_target="tpu_custom_call" | custom-call | tf_op jit(solution)/shard_map/pallas_call | solution.py:406
  29.1 1.0 %copy.6 = bf16[64,8192]{1,0:T(8,128)(2,1)} copy(bf16[64,8192]{1,0:T(8,128)(2,1)S(1)} %shard_map.46) | data formatting | bytes 2097152

commit v3 on v2

--- a/solution.py
+++ b/solution.py
@@ -35,7 +35,6 @@
     d = HEAD_WIDTH
     chips = ny * nx
     both = 2 * rows
-    keys = chips * both
     half = kinds * group * d
     z = lax.axis_index("outer")
     inner = lax.axis_index("inner")
@@ -225,8 +224,10 @@
                 arrived_if(more, n, last, sl)
                 pass_on("values", n, last, sl, sl, n_there, more, zz=there)
 
-    def gather(n, piece):
-        for sl in ([0] if n == 0 else []) + along_x + along_y + corner:
+    def gather(n, piece, slots):
+        for sl in slots:
+            if n and not sl:
+                continue
             if on_line(n, piece):
                 arrived_if(jnp.logical_not(farther(n)[2]), n, piece, sl)
             else:
@@ -235,9 +236,9 @@
     def positions_of(n, sl):
         return jnp.concatenate([pbuf[n, sl, 0], pbuf[n, sl, 1]], axis=1).astype(jnp.float32)
 
-    def build_mask(n):
+    def build_mask(n, slots):
         mine = jnp.broadcast_to(positions_of(0, 0), (both, both))
-        for sl in range(chips):
+        for sl in slots:
             theirs = jnp.broadcast_to(positions_of(n, sl), (both, both)).T
             mask[n, sl * both:(sl + 1) * both, :] = jnp.where(
                 theirs > mine, HIDDEN, 0.0).astype(jnp.bfloat16)
@@ -251,14 +252,14 @@
     per_tile = math.gcd(max(1, 512 // rows), group)
     tile = per_tile * rows
     tiles = [(owner, t) for owner in (1, 0) for t in range(group // per_tile)]
-    ones = jnp.ones((keys, d), jnp.bfloat16)
 
     def column(kind, t, j):
         return (kind * group + t * per_tile + j) * d
 
-    def score(n, kind, i):
+    def score(n, kind, lo, hi, i):
         owner, t = tiles[i]
-        k_wide = jnp.concatenate([buf[n, 2 * kind].reshape(keys, d), mask[n]], axis=1)
+        k_wide = jnp.concatenate([buf[n, 2 * kind, lo:hi].reshape((hi - lo) * both, d),
+                                  mask[n, lo * both:hi * both, :]], axis=1)
         query = jnp.concatenate(
             [jnp.concatenate([q_buf[owner * rows:(owner + 1) * rows,
                                     column(kind, t, j):column(kind, t, j) + d], picks[owner]],
@@ -267,12 +268,15 @@
         return lax.dot_general(query, k_wide, (((1,), (1,)), ((), ())),
                                preferred_element_type=jnp.float32)
 
-    def fold(n, kind, i, scores):
+    def fold(n, kind, lo, hi, i, scores):
         owner, t = tiles[i]
-        v_wide = jnp.concatenate([buf[n, 2 * kind + 1].reshape(keys, d), ones], axis=1)
+        keys = (hi - lo) * both
+        later = n or lo
+        v_wide = jnp.concatenate([buf[n, 2 * kind + 1, lo:hi].reshape(keys, d),
+                                  jnp.ones((keys, d), jnp.bfloat16)], axis=1)
         window = slice(i * tile, (i + 1) * tile)
         new_top = jnp.broadcast_to(jnp.max(scores, axis=1, keepdims=True), (tile, d))
-        if n:
+        if later:
             old_top = top[kind, window, :]
             new_top = jnp.maximum(old_top, new_top)
             rescale = jnp.exp2((old_top - new_top) * scale)
@@ -280,9 +284,9 @@
                            * scale).astype(jnp.bfloat16)
         got = lax.dot_general(weights, v_wide, (((1,), (0,)), ((), ())),
                               preferred_element_type=jnp.float32)
-        if n:
+        if later:
             got = acc[kind, window, :] * jnp.concatenate([rescale, rescale], axis=1) + got
-        if n < nz - 1:
+        if n < nz - 1 or hi < chips:
             acc[kind, window, :] = got
             top[kind, window, :] = new_top
             return
@@ -309,73 +313,91 @@
                     what(n, POS)
                 what(n, piece)
 
-    def ready(i):
-        n, kind = divmod(i, 2)
-        for piece in ((POS, 0, 1), (2, 3))[kind]:
-            gather(n, piece)
-        if kind == 0:
-            build_mask(n)
-
     def line_values(n, slots):
         if n <= half_way:
             values(n, slots)
 
-    def between(i):
-        if i == 0:
+    def first_actions():
+        for piece in range(PIECES):
+            at(along, 1, (piece,))
+            at(across, 1, (piece,))
+            at(along, 2, (piece,))
+            if piece > 1:
+                at(relay, 0, (piece,))
+        at(relay, 0, (1, 0))
+        at(across, 2, (0,))
+        values(0, along_x)
+
+    def after(step):
+        n, kind, lo, hi = step
+        if n == 0 and kind == 0 and lo == 0:
+            at(along, 3, (0, 1))
+            at(across, 2, (1,))
+            at(relay, 1, (1,))
+            at(along, 3, (2,))
+            at(relay, 1, (0,))
+            values(0, along_y)
+        elif n == 0 and lo == 0:
+            at(across, 2, (2,))
             at(along, 3, (3,))
+            at(across, 2, (3,))
+            at(relay, 1, (2,))
+            values(0, corner)
+        elif n == 0 and kind == 0:
+            line_values(2, along_x)
+            at(across, 3, (0,))
+            at(relay, 2, (1, 0))
+            at(across, 3, (1,))
+        elif n == 0:
+            at(across, 3, (2,))
+            line_values(1, along_x + along_y)
+            line_values(2, along_y)
+        elif n == 1 and kind == 0:
+            at(relay, 2, (2,))
+            line_values(2, corner)
+            at(across, 3, (3,))
+            line_values(1, corner)
             at(relay, 1, (3,))
-            values(0, corner)
-            at(across, 3, (0, 1))
-            at(relay, 2, (0, 1))
-            line_values(1, along_x + along_y)
-        if i == 1:
-            at(across, 3, (2, 3))
-            at(relay, 2, (2, 3))
-            line_values(2, along_x + along_y)
-            line_values(1, corner)
-        if i == 2:
+            at(relay, 2, (3,))
+        elif n == 1:
             at(relay, 3, (0, 1))
-            line_values(2, corner)
-        if i == 3:
+        elif n == 2 and kind == 0:
             at(relay, 3, (2, 3))
-        if i % 2:
+        if n and kind:
             for what in (along, across, relay):
-                at(what, i // 2 + 4, range(PIECES))
-
-    for piece in range(PIECES):
-        at(along, 1, (piece,))
-        at(across, 1, (piece,))
-        at(along, 2, (piece,))
-        at(relay, 0, (piece,))
-    for piece in range(PIECES - 1):
-        at(across, 2, (piece,))
-        at(along, 3, (piece,))
-        at(relay, 1, (piece,))
-        if piece:
-            values(0, along_y if piece == 1 else along_x)
-    at(across, 2, (PIECES - 1,))
+                at(what, n + 3, range(PIECES))
+
+    def ready(step):
+        n, kind, lo, hi = step
+        for piece in ((POS, 0, 1), (2, 3))[kind]:
+            gather(n, piece, range(lo, hi))
+        if kind == 0:
+            build_mask(n, range(lo, hi))
+
+    first_actions()
     q_copy.wait()
     landed(q_buf.at[pl.ds(rows, rows)], q_sem)
 
+    steps = [(0, kind, lo, hi) for lo, hi in ((0, nx), (nx, chips)) for kind in range(2)]
+    steps += [(n, kind, 0, chips) for n in range(1, nz) for kind in range(2)]
     ours = len(tiles) // 2
-    work = [(n, kind, i) for n in range(nz - 1) for kind in range(2) for i in range(len(tiles))]
-    last = [(kind, i) for kind in range(2) for i in range(len(tiles))]
-    late = [(0, len(tiles) - 1)] + [(1, i) for i in range(ours, len(tiles))]
-    work += [(nz - 1,) + w for w in last if w not in late] + [(nz - 1,) + w for w in late]
+    work = [step + (i,) for step in steps[:-2] for i in range(len(tiles))]
+    work += [step + (i,) for step in steps[-2:] for i in range(ours)]
+    late = [step + (i,) for step in steps[-2:] for i in range(ours, len(tiles))]
+    work += late
     begun = 0
-    ready(0)
+    ready(steps[0])
     held = score(*work[0])
     for w, task in enumerate(work):
         following = None
         if w + 1 < len(work):
-            step = 2 * work[w + 1][0] + work[w + 1][1]
+            step = steps.index(work[w + 1][:-1])
             if step > begun:
-                between(begun)
+                after(steps[begun])
                 begun = step
-                ready(step)
-                if step == 2 * nz - 1:
-                    swap(0)
-            if work[w + 1] == (nz - 1,) + late[1]:
+                ready(steps[step])
+            if work[w + 1] == late[1]:
+                swap(0)
                 swap(1)
             following = score(*work[w + 1])
         fold(*task, held)

time: 30.2 us -> 29.2 us (0.967)
  Pallas kernels: 29.1 us -> 28 us
    pallas_call x1, Pallas kernels: 29.1 us -> 28 us  [body(): pl.pallas_call(functools.partial(kernel, sizes), out_shape=pltpu.VMEM((ro...]
where the time goes in v3:
time: 29.2 us; the launch traced here: 29 us
  Pallas kernels  28 us (96%)
  local copies, waits for them, and re-layouts  0.97 us (3%)
    pallas_call x1, Pallas kernels, body(): pl.pallas_call(functools.partial(kernel, sizes), out_shape=pltpu.VMEM((ro...  28 us
    unnamed x1, local copies, waits for them, and re-layouts  0.97 us

profile of v3, /device:TPU:0, one launch (start us, length us, event | category | flops | bytes accessed | tf_op | source)
XLA Modules:
  0.0 29.0 jit_solution(2736142149199207359)
XLA Ops:
  0.0 28.0 %shard_map.46 = bf16[64,8192]{1,0:T(8,128)(2,1)S(1)} custom-call(bf16[64,8192]{1,0:T(8,128)(2,1)} %q_ref.1, bf16[64,512]{1,0:T(8,128)(2,1)} %k_ref.1, bf16[64,512]{1,0:T(8,128)(2,1)} %v_ref.1, s32[1,64]{1,0:T(1,128)} %bitcast.1), custom_call_target="tpu_custom_call" | custom-call | tf_op jit(solution)/shard_map/pallas_call | solution.py:428
  28.0 1.0 %copy.6 = bf16[64,8192]{1,0:T(8,128)(2,1)} copy(bf16[64,8192]{1,0:T(8,128)(2,1)S(1)} %shard_map.46) | data formatting | bytes 2097152

commit v4 on v3

--- a/solution.py
+++ b/solution.py
@@ -325,14 +325,14 @@
             if piece > 1:
                 at(relay, 0, (piece,))
         at(relay, 0, (1, 0))
-        at(across, 2, (0,))
-        values(0, along_x)
 
     def after(step):
         n, kind, lo, hi = step
         if n == 0 and kind == 0 and lo == 0:
+            at(across, 2, (0,))
+            values(0, along_x)
+            at(across, 2, (1,))
             at(along, 3, (0, 1))
-            at(across, 2, (1,))
             at(relay, 1, (1,))
             at(along, 3, (2,))
             at(relay, 1, (0,))

time: 29.2 us -> 29.2 us (level)
  no operation moved by 1% of the time
where the time goes in v4:
time: 29.2 us; the launch traced here: 29 us
  Pallas kernels  28 us (96%)
  local copies, waits for them, and re-layouts  0.97 us (3%)
    pallas_call x1, Pallas kernels, body(): pl.pallas_call(functools.partial(kernel, sizes), out_shape=pltpu.VMEM((ro...  28 us
    unnamed x1, local copies, waits for them, and re-layouts  0.97 us

profile of v4, /device:TPU:0, one launch (start us, length us, event | category | flops | bytes accessed | tf_op | source)
XLA Modules:
  0.0 29.0 jit_solution(18052853075268450788)
XLA Ops:
  0.0 28.0 %shard_map.46 = bf16[64,8192]{1,0:T(8,128)(2,1)S(1)} custom-call(bf16[64,8192]{1,0:T(8,128)(2,1)} %q_ref.1, bf16[64,512]{1,0:T(8,128)(2,1)} %k_ref.1, bf16[64,512]{1,0:T(8,128)(2,1)} %v_ref.1, s32[1,64]{1,0:T(1,128)} %bitcast.1), custom_call_target="tpu_custom_call" | custom-call | tf_op jit(solution)/shard_map/pallas_call | solution.py:428
  28.0 1.0 %copy.6 = bf16[64,8192]{1,0:T(8,128)(2,1)} copy(bf16[64,8192]{1,0:T(8,128)(2,1)S(1)} %shard_map.46) | data formatting | bytes 2097152
